TPU v7x, 32 devices: a whole 2x2x4 slice. The times are simulated.
32 devices in a mesh: pr: 8 (over y, x, core), pc: 4 (over z).
Axes of the slice: x: 2, y: 2, z: 4, core: 2. Of those that a mesh axis runs over, the one named last changes fastest.
Arguments:
- pair_array: bfloat16 [256, 256, 128], P('pr', 'pc'), may hold values from -6 to 6
- left_weight: bfloat16 [128, 128], replicated, may hold values from -0.5 to 0.5
- right_weight: bfloat16 [128, 128], replicated, may hold values from -0.5 to 0.5
- left_gate: bfloat16 [128, 128], replicated, may hold values from -0.5 to 0.5
- right_gate: bfloat16 [128, 128], replicated, may hold values from -0.5 to 0.5
- mid_gain: float32 [128], replicated, may hold values from 0.25 to 1.75
- out_weight: bfloat16 [128, 128], replicated, may hold values from -0.5 to 0.5
- out_gate: bfloat16 [128, 128], replicated, may hold values from -0.5 to 0.5
Outputs:
- pair_update: bfloat16 [256, 256, 128], P('pr', 'pc')
All inputs are finite; a program needn't handle non-finite values.
Results may differ from a plain program's by a relative error of at most 0.012.
Values may be sent and summed in bfloat16 or wider, within the bound.
A program may use at most 128 MiB of HBM per device.

v0:
```python
import functools

import jax
import jax.numpy as jnp
from jax import lax
from jax.experimental import pallas as pl
from jax.experimental.pallas import tpu as pltpu
from jax.sharding import PartitionSpec as P

MESH = pl.DeviceIdType.MESH
BF16 = jnp.bfloat16
F32 = jnp.float32
LANES = 128
SUB = 16
UF, UP, UE = 16, 8, 16


def unit_channels(values, channel_gain):
    centred = values - jnp.mean(values, axis=-1, keepdims=True)
    return (
        centred
        * lax.rsqrt(jnp.mean(centred * centred, axis=-1, keepdims=True) + 1e-05)
        * channel_gain
    )


def make_factors(pair_in, left_weight, right_weight, left_gate, right_gate):
    left = jnp.einsum("ijc,cd->ijd", pair_in, left_weight, preferred_element_type=F32)
    left = left * jax.nn.sigmoid(
        jnp.einsum("ijc,cd->ijd", pair_in, left_gate, preferred_element_type=F32)
    )
    right = jnp.einsum("ijc,cd->ijd", pair_in, right_weight, preferred_element_type=F32)
    right = right * jax.nn.sigmoid(
        jnp.einsum("ijc,cd->ijd", pair_in, right_gate, preferred_element_type=F32)
    )
    return (pair_in, left.astype(BF16), right.astype(BF16))


def to_pair(mixed, ready, mid_gain, out_weight, out_gate):
    scaled = unit_channels(mixed.astype(F32), mid_gain).astype(BF16)
    scaled = lax.optimization_barrier(scaled)
    gate = jax.nn.sigmoid(jnp.einsum("ijc,cd->ijd", ready, out_gate, preferred_element_type=F32))
    return (
        jnp.einsum("ijd,dc->ijc", scaled, out_weight, preferred_element_type=F32) * gate
    ).astype(BF16)


def plain(
    pair_array, left_weight, right_weight, left_gate, right_gate, mid_gain, out_weight, out_gate
):
    ready, left, right = make_factors(pair_array, left_weight, right_weight, left_gate, right_gate)
    count = pair_array.shape[0] * lax.axis_size("pr")
    left_lines, right_lines = (
        lax.all_to_all(left, "pr", split_axis=2, concat_axis=0, tiled=True),
        lax.all_to_all(right, "pr", split_axis=2, concat_axis=0, tiled=True),
    )
    strip = jnp.einsum(
        "kid,kjd->ijd",
        lax.all_gather(left_lines, "pc", axis=1, tiled=True),
        right_lines,
        preferred_element_type=F32,
    )
    strip = (strip * count ** (-0.5)).astype(BF16)
    mixed = lax.all_to_all(strip, "pr", split_axis=0, concat_axis=2, tiled=True)
    return to_pair(mixed, ready, mid_gain, out_weight, out_gate)


def nt(a, b):
    return lax.dot_general(a, b, (((1,), (1,)), ((), ())), preferred_element_type=F32)


def tn(a, b):
    return lax.dot_general(a, b, (((0,), (0,)), ((), ())), preferred_element_type=F32)


GROUPS = ((0, 0), (0, 1), (1, 0), (1, 1))


def kernel(
    n_p, n_q, x_hbm, lw_hbm, rw_hbm, lg_hbm, rg_hbm, gain_hbm, ow_hbm, og_hbm, out_ref,
    x_ref, lw_ref, rw_ref, lg_ref, rg_ref, gain_ref, ow_ref, og_ref, in_s,
    turn, lsend, rsend, lrecv, rrecv, osend, orecv, gate,
    l_ss, l_rs, r_ss, r_rs, o_ss, o_rs,
):
    p = lax.axis_index("pr")
    q = lax.axis_index("pc")
    zh = q // 2
    zl = q % 2
    me = p * 2 + zl
    n_e = n_p * 2
    per = lsend.shape[1] // SUB
    width = x_ref.shape[1]
    rows = x_ref.shape[0] // 2
    channels = n_e * per
    count = n_p * x_ref.shape[0]

    brought = [
        pltpu.make_async_copy(src, dst, in_s.at[at])
        for at, (src, dst) in enumerate(
            (
                (x_hbm, x_ref), (rw_hbm, rw_ref), (rg_hbm, rg_ref), (lw_hbm, lw_ref),
                (lg_hbm, lg_ref), (og_hbm, og_ref), (ow_hbm, ow_ref), (gain_hbm, gain_ref),
            )
        )
    ]
    for copy in brought:
        copy.start()

    barrier = pltpu.get_barrier_semaphore()
    for dp in range(n_p):
        for dh, dl in GROUPS:
            if (dp, dh, dl) != (0, 0, 0):
                to = (lax.rem(p + dp, n_p), lax.rem(zh + dh, 2) * 2 + lax.rem(zl + dl, 2))
                pl.semaphore_signal(barrier, inc=1, device_id=to, device_id_type=MESH)

    def pair_rows(k):
        return jnp.concatenate([x_ref[k], x_ref[k + rows]], axis=0)

    def factor(w_ref, g_ref, send):
        both = jnp.concatenate([w_ref[...].T, g_ref[...].T], axis=0)

        def step(k, _):
            pr = nt(both, pair_rows(k))
            turn[pl.ds(k, channels, stride=SUB), :] = pr[:channels] * jax.nn.sigmoid(pr[channels:])
            return 0

        lax.fori_loop(0, rows, step, 0, unroll=UF)

        def cast(e, _):
            at = pl.multiple_of(e * per * SUB, per * SUB)
            send[e] = turn[pl.ds(at, per * SUB), :].astype(BF16)
            return 0

        lax.fori_loop(0, n_e, cast, 0, unroll=4)

    def r_copy(dp, dl, arriving=False):
        to_p, to_l = lax.rem(p + dp, n_p), lax.rem(zl + dl, 2)
        return pltpu.make_async_remote_copy(
            src_ref=rsend.at[to_p * 2 + to_l],
            dst_ref=rrecv.at[dl, dp],
            send_sem=r_ss.at[dl, dp],
            recv_sem=r_rs.at[dl, dp],
            device_id=(to_p, zh * 2 + to_l),
            device_id_type=MESH,
        )

    def l_copy(dp, group):
        dh, dl = GROUPS[group]
        to_p, to_l = lax.rem(p + dp, n_p), lax.rem(zl + dl, 2)
        return pltpu.make_async_remote_copy(
            src_ref=lsend.at[to_p * 2 + to_l],
            dst_ref=lrecv.at[group, dp],
            send_sem=l_ss.at[group, dp],
            recv_sem=l_rs.at[group, dp],
            device_id=(to_p, lax.rem(zh + dh, 2) * 2 + to_l),
            device_id_type=MESH,
        )

    for copy in brought:
        copy.wait()
    factor(rw_ref, rg_ref, rsend)
    pl.semaphore_wait(barrier, n_p * n_q - 1)
    for dl in (1, 0):
        for dp in range(n_p):
            if (dp, dl) != (0, 0):
                r_copy(dp, dl).start()
    factor(lw_ref, lg_ref, lsend)
    for group in range(4):
        for dp in range(n_p):
            if (dp, group) != (0, 0):
                l_copy(dp, group).start()
    rrecv[0, 0] = rsend[me]
    lrecv[0, 0] = lsend[me]

    def make_gate(k, _):
        gate[k] = jax.nn.sigmoid(
            jnp.dot(pair_rows(k), og_ref[...], preferred_element_type=F32)
        )
        return 0

    lax.fori_loop(0, rows, make_gate, 0, unroll=4)

    for dl in (1, 0):
        for dp in range(n_p):
            if (dp, dl) != (0, 0):
                r_copy(dp, dl).wait_recv()

    low = lax.broadcasted_iota(jnp.int32, (SUB, LANES), 1) < width

    def o_copy(group, b, dl):
        dh, gl = GROUPS[group]
        z = lax.rem(zh + dh, 2) * 2 + lax.rem(zl + gl, 2)
        to_p, to_l = z * 2 + b, lax.rem(zl + dl, 2)
        away = (to_p != p) if dl == 0 else None
        return away, pltpu.make_async_remote_copy(
            src_ref=osend.at[group, b, dl],
            dst_ref=orecv.at[me],
            send_sem=o_ss.at[group, b, dl],
            recv_sem=o_rs.at[me],
            device_id=(to_p, zh * 2 + to_l),
            device_id_type=MESH,
        )

    for group in range(4):
        for dp in range(n_p):
            if (dp, group) != (0, 0):
                l_copy(dp, group).wait_recv()

        def products(d, _):
            at = pl.ds(pl.multiple_of(d * SUB, SUB), SUB)
            left = lrecv[group, :, at, :].reshape(n_p * SUB, LANES)
            right = [rrecv[dl, :, at, :].reshape(n_p * SUB, LANES) for dl in range(2)]
            sums = tn(left, jnp.concatenate(right, axis=1))
            for dl in range(2):
                acc = sums[:, dl * LANES : (dl + 1) * LANES]
                for b in range(2):
                    top = b * 2 * SUB
                    a0, c0 = acc[top : top + SUB], acc[top + SUB : top + 2 * SUB]
                    b0 = acc[width + top : width + top + SUB]
                    d0 = acc[width + top + SUB : width + top + 2 * SUB]
                    tile = jnp.where(low, a0, d0) + pltpu.roll(
                        jnp.where(low, c0, b0), width, 1
                    )
                    osend[group, b, dl, at, :] = (tile * count ** (-0.5)).astype(BF16)
            return 0

        lax.fori_loop(0, per, products, 0, unroll=UP)
        for b in range(2):
            for dl in (1, 0):
                away, copy = o_copy(group, b, dl)
                if away is None:
                    copy.start()
                else:

                    @pl.when(away)
                    def _():
                        copy.start()

                    @pl.when(jnp.logical_not(away))
                    def _():
                        orecv[me] = osend[group, b, dl]

    gain = jnp.broadcast_to(gain_ref[...], (channels, channels)).T
    for off in range(1, n_e):
        at = lax.rem(me + off, n_e)
        pltpu.make_async_remote_copy(
            src_ref=osend.at[0, 0, 0],
            dst_ref=orecv.at[at],
            send_sem=o_ss.at[0, 0, 0],
            recv_sem=o_rs.at[at],
            device_id=(p, q),
            device_id_type=MESH,
        ).wait_recv()

    def widen(e, _):
        at = pl.multiple_of(e * per * SUB, per * SUB)
        turn[pl.ds(at, per * SUB), :] = orecv[e].astype(F32)
        return 0

    lax.fori_loop(0, n_e, widen, 0, unroll=4)

    def finish(k, _):
        v = turn[pl.ds(k, channels, stride=SUB), :]
        v = v - jnp.mean(v, axis=0, keepdims=True)
        v = v * lax.rsqrt(jnp.mean(v * v, axis=0, keepdims=True) + 1e-05) * gain
        res = (tn(v.astype(BF16), ow_ref[...]) * gate[k]).astype(BF16)
        out_ref[k] = res[:width]
        out_ref[k + rows] = res[width:]
        return 0

    lax.fori_loop(0, rows, finish, 0, unroll=UE)

    for dl in range(2):
        for dp in range(n_p):
            if (dp, dl) != (0, 0):
                r_copy(dp, dl).wait_send()
    for group in range(4):
        for dp in range(n_p):
            if (dp, group) != (0, 0):
                l_copy(dp, group).wait_send()
        for b in range(2):
            for dl in range(2):
                away, copy = o_copy(group, b, dl)
                if away is None:
                    copy.wait_send()
                else:

                    @pl.when(away)
                    def _():
                        copy.wait_send()


def fused(n_p, n_q, pair_array, lw, rw, lg, rg, gain, ow, og):
    channels = lw.shape[1]
    n_e = n_p * 2
    slab = channels // n_e * SUB
    rows = pair_array.shape[0] // 2
    dma = pltpu.SemaphoreType.DMA
    return pl.pallas_call(
        functools.partial(kernel, n_p, n_q),
        out_shape=jax.ShapeDtypeStruct(pair_array.shape, BF16),
        in_specs=[pl.BlockSpec(memory_space=pltpu.HBM)] * 8,
        out_specs=pl.BlockSpec(memory_space=pltpu.VMEM),
        scratch_shapes=[
            pltpu.VMEM(pair_array.shape, BF16),
            *[pltpu.VMEM(lw.shape, BF16)] * 4,
            pltpu.VMEM((1, channels), F32),
            pltpu.VMEM(ow.shape, BF16),
            pltpu.VMEM(og.shape, BF16),
            dma((8,)),
            pltpu.VMEM((channels * SUB, LANES), F32),
            pltpu.VMEM((n_e, slab, LANES), BF16),
            pltpu.VMEM((n_e, slab, LANES), BF16),
            pltpu.VMEM((4, n_p, slab, LANES), BF16),
            pltpu.VMEM((2, n_p, slab, LANES), BF16),
            pltpu.VMEM((4, 2, 2, slab, LANES), BF16),
            pltpu.VMEM((n_e, slab, LANES), BF16),
            pltpu.VMEM((rows, LANES, channels), F32),
            dma((4, n_p)),
            dma((4, n_p)),
            dma((2, n_p)),
            dma((2, n_p)),
            dma((4, 2, 2)),
            dma((n_e,)),
        ],
        compiler_params=pltpu.CompilerParams(
            collective_id=0, has_side_effects=True, vmem_limit_bytes=67_043_328
        ),
    )(pair_array, lw, rw, lg, rg, gain.reshape(1, channels), ow, og)


def solution(mesh):
    n_p, n_q = mesh.shape["pr"], mesh.shape["pc"]

    def on_device(pair_array, lw, *rest):
        first, second, wide = pair_array.shape
        fits = (
            n_q == 4
            and first == 2 * SUB
            and second == 2 * first
            and n_p == 2 * n_q
            and 2 * second == LANES
            and wide == LANES
            and lw.shape[1] == LANES
        )
        if fits:
            return fused(n_p, n_q, pair_array, lw, *rest)
        return plain(pair_array, lw, *rest)

    return jax.shard_map(
        on_device,
        mesh=mesh,
        in_specs=(P("pr", "pc", None), P(), P(), P(), P(), P(), P(), P()),
        out_specs=P("pr", "pc", None),
        check_vma=False,
    )
```

profile of v0, /device:TPU:7, one launch (start us, length us, event | category | flops | bytes accessed | tf_op | source)
XLA Modules:
  0.0 42.1 jit_solution(7699986066489069951)
XLA Ops:
  0.0 40.2 %shard_map.82 = bf16[32,64,128]{2,1,0:T(8,128)(2,1)} custom-call(bf16[32,64,128]{2,1,0:T(8,128)(2,1)} %x_hbm.1, bf16[128,128]{1,0:T(8,128)(2,1)} %lw_hbm.1, bf16[128,128]{1,0:T(8,128)(2,1)} %rw_hbm.1, bf16[128,128]{1,0:T(8,128)(2,1)} %lg_hbm.1, bf16[128,128]{1,0:T(8,128)(2,1)} %rg_hbm.1, f32[1,128]{1,0:T(1,128)} %bitcast.1, bf16[128,128]{1,0:T(8,128)(2,1)} %ow_hbm.1, ...), custom_call_target="tpu_custom_call" | custom-call | tf_op jit(solution)/shard_map/pallas_call | solution.py:299
  40.2 1.9 %copy.10 = bf16[32,64,128]{2,1,0:T(8,128)(2,1)} copy(bf16[32,64,128]{2,1,0:T(8,128)(2,1)} %shard_map.82) | data formatting | bytes 1048576
where the time goes:
time: 42.2 us; the launch traced here: 42.1 us
  Pallas kernels  40.2 us (95%)
  local copies, waits for them, and re-layouts  1.87 us (4%)
    pallas_call x1, Pallas kernels, fused(): pl.pallas_call(functools.partial(kernel, n_p, n_q), out_shape=jax.ShapeDt...  40.2 us
    unnamed x1, local copies, waits for them, and re-layouts  1.87 us

commit v1 on v0

--- a/solution.py
+++ b/solution.py
@@ -241,6 +241,14 @@
                         orecv[me] = osend[group, b, dl]
 
     gain = jnp.broadcast_to(gain_ref[...], (channels, channels)).T
+    for dl in range(2):
+        for dp in range(n_p):
+            if (dp, dl) != (0, 0):
+                r_copy(dp, dl).wait_send()
+    for group in range(4):
+        for dp in range(n_p):
+            if (dp, group) != (0, 0):
+                l_copy(dp, group).wait_send()
     for off in range(1, n_e):
         at = lax.rem(me + off, n_e)
         pltpu.make_async_remote_copy(
@@ -270,14 +278,7 @@
 
     lax.fori_loop(0, rows, finish, 0, unroll=UE)
 
-    for dl in range(2):
-        for dp in range(n_p):
-            if (dp, dl) != (0, 0):
-                r_copy(dp, dl).wait_send()
     for group in range(4):
-        for dp in range(n_p):
-            if (dp, group) != (0, 0):
-                l_copy(dp, group).wait_send()
         for b in range(2):
             for dl in range(2):
                 away, copy = o_copy(group, b, dl)
@@ -298,7 +299,7 @@
     dma = pltpu.SemaphoreType.DMA
     return pl.pallas_call(
         functools.partial(kernel, n_p, n_q),
-        out_shape=jax.ShapeDtypeStruct(pair_array.shape, BF16),
+        out_shape=pltpu.VMEM(pair_array.shape, BF16),
         in_specs=[pl.BlockSpec(memory_space=pltpu.HBM)] * 8,
         out_specs=pl.BlockSpec(memory_space=pltpu.VMEM),
         scratch_shapes=[
@@ -324,9 +325,12 @@
             dma((n_e,)),
         ],
         compiler_params=pltpu.CompilerParams(
-            collective_id=0, has_side_effects=True, vmem_limit_bytes=67_043_328
+            collective_id=0, has_side_effects=True, vmem_limit_bytes=33_554_432
         ),
-    )(pair_array, lw, rw, lg, rg, gain.reshape(1, channels), ow, og)
+    )(*(
+        pltpu.with_memory_space_constraint(a, pltpu.HBM)
+        for a in (pair_array, lw, rw, lg, rg, gain.reshape(1, channels), ow, og)
+    ))
 
 
 def solution(mesh):

time: 42.2 us -> 40.3 us (0.955)
  local copies, waits for them, and re-layouts: 1.87 us -> 0.8 us
  Pallas kernels: 40.2 us -> 39.3 us
    unnamed x1, local copies, waits for them, and re-layouts: 1.87 us -> 0.8 us
    pallas_call x1, Pallas kernels: 40.2 us -> 39.3 us  [fused(): pl.pallas_call(functools.partial(kernel, n_p, n_q), out_shape=pltpu.VMEM(...]
where the time goes in v1:
time: 40.3 us; the launch traced here: 40.1 us
  Pallas kernels  39.3 us (98%)
  local copies, waits for them, and re-layouts  0.8 us (2%)
    pallas_call x1, Pallas kernels, fused(): pl.pallas_call(functools.partial(kernel, n_p, n_q), out_shape=pltpu.VMEM(...  39.3 us

profile of v1, /device:TPU:7, one launch (start us, length us, event | category | flops | bytes accessed | tf_op | source)
XLA Modules:
  0.0 40.1 jit_solution(8435201004115353090)
XLA Ops:
  0.0 39.3 %shard_map.82 = bf16[32,64,128]{2,1,0:T(8,128)(2,1)S(1)} custom-call(bf16[32,64,128]{2,1,0:T(8,128)(2,1)} %x_hbm.1, bf16[128,128]{1,0:T(8,128)(2,1)} %lw_hbm.1, bf16[128,128]{1,0:T(8,128)(2,1)} %rw_hbm.1, bf16[128,128]{1,0:T(8,128)(2,1)} %lg_hbm.1, bf16[128,128]{1,0:T(8,128)(2,1)} %rg_hbm.1, f32[1,128]{1,0:T(1,128)} %bitcast.1, bf16[128,128]{1,0:T(8,128)(2,1)} %ow_hbm.1, ...), custom_call_target="tpu_custom_call" | custom-call | tf_op jit(solution)/shard_map/pallas_call | solution.py:300
  39.3 0.8 %copy.10 = bf16[32,64,128]{2,1,0:T(8,128)(2,1)} copy(bf16[32,64,128]{2,1,0:T(8,128)(2,1)S(1)} %shard_map.82) | data formatting | bytes 1048576

commit v2 on v1

v2 whole, which is shorter than its diff:
```python
import functools

import jax
import jax.numpy as jnp
from jax import lax
from jax.experimental import pallas as pl
from jax.experimental.pallas import tpu as pltpu
from jax.sharding import PartitionSpec as P

MESH = pl.DeviceIdType.MESH
BF16 = jnp.bfloat16
F32 = jnp.float32
LANES = 128
SUB = 16
UF, UP, UE = 16, 8, 16


def unit_channels(values, channel_gain):
    centred = values - jnp.mean(values, axis=-1, keepdims=True)
    return (
        centred
        * lax.rsqrt(jnp.mean(centred * centred, axis=-1, keepdims=True) + 1e-05)
        * channel_gain
    )


def make_factors(pair_in, left_weight, right_weight, left_gate, right_gate):
    left = jnp.einsum("ijc,cd->ijd", pair_in, left_weight, preferred_element_type=F32)
    left = left * jax.nn.sigmoid(
        jnp.einsum("ijc,cd->ijd", pair_in, left_gate, preferred_element_type=F32)
    )
    right = jnp.einsum("ijc,cd->ijd", pair_in, right_weight, preferred_element_type=F32)
    right = right * jax.nn.sigmoid(
        jnp.einsum("ijc,cd->ijd", pair_in, right_gate, preferred_element_type=F32)
    )
    return (pair_in, left.astype(BF16), right.astype(BF16))


def to_pair(mixed, ready, mid_gain, out_weight, out_gate):
    scaled = unit_channels(mixed.astype(F32), mid_gain).astype(BF16)
    scaled = lax.optimization_barrier(scaled)
    gate = jax.nn.sigmoid(jnp.einsum("ijc,cd->ijd", ready, out_gate, preferred_element_type=F32))
    return (
        jnp.einsum("ijd,dc->ijc", scaled, out_weight, preferred_element_type=F32) * gate
    ).astype(BF16)


def plain(
    pair_array, left_weight, right_weight, left_gate, right_gate, mid_gain, out_weight, out_gate
):
    ready, left, right = make_factors(pair_array, left_weight, right_weight, left_gate, right_gate)
    count = pair_array.shape[0] * lax.axis_size("pr")
    left_lines, right_lines = (
        lax.all_to_all(left, "pr", split_axis=2, concat_axis=0, tiled=True),
        lax.all_to_all(right, "pr", split_axis=2, concat_axis=0, tiled=True),
    )
    strip = jnp.einsum(
        "kid,kjd->ijd",
        lax.all_gather(left_lines, "pc", axis=1, tiled=True),
        right_lines,
        preferred_element_type=F32,
    )
    strip = (strip * count ** (-0.5)).astype(BF16)
    mixed = lax.all_to_all(strip, "pr", split_axis=0, concat_axis=2, tiled=True)
    return to_pair(mixed, ready, mid_gain, out_weight, out_gate)


def nt(a, b):
    return lax.dot_general(a, b, (((1,), (1,)), ((), ())), preferred_element_type=F32)


def tn(a, b):
    return lax.dot_general(a, b, (((0,), (0,)), ((), ())), preferred_element_type=F32)


HOME = (3, 3)
MOVED = (4, 4, 2)
CHUNKS = HOME + MOVED
ORDER = ('M', 'N0', 'N1', 'O', 'g', 'F0', 'N2', 'C0', 'F1', 'N3', 'C1', 'N4', 'F2', 'D0', 'P0', 'Q0', 'C2', 'P2', 'D1', 'P1', 'Q1', 'F3', 'C3', 'P3', 'F4', 'D2', 'Q2', 'C4', 'P4', 'D3', 'Q3', 'D4', 'Q4')


def kernel(
    n_p, n_q, x_hbm, lw_hbm, rw_hbm, lg_hbm, rg_hbm, gain_hbm, ow_hbm, og_hbm, out_ref,
    x_ref, lw_ref, rw_ref, lg_ref, rg_ref, gain_ref, ow_ref, og_ref, in_s,
    turn, lsend, rsend, lbuf, rbuf, osend, orecv, gate,
    a_ss, a_rs, f_ss, own_rs, f_rs, e_ss, e_rs, o_ss, o_rs,
):
    p = lax.axis_index("pr")
    q = lax.axis_index("pc")
    half = q // 2
    mid, end = 1 + half, 3 * half
    far_mid, far_end = 2 - half, 3 - 3 * half
    at_mid = q == mid
    per = lsend.shape[1] // SUB
    width = x_ref.shape[1]
    rows = x_ref.shape[0] // 2
    channels = n_p * per
    count = n_p * x_ref.shape[0]
    planes = (mid, end, far_mid, far_end)
    n_c = len(CHUNKS)
    part = [pl.ds(sum(CHUNKS[:c]) * SUB, CHUNKS[c] * SUB) for c in range(n_c)]
    others = pl.ds(1, n_p - 1)
    pair = pl.ds(0, 2)
    away = pl.ds(2, n_p - 2)
    n_h = len(HOME)
    home = pl.ds(0, sum(HOME) * SUB)
    moved = pl.ds(sum(HOME) * SUB, sum(MOVED) * SUB)

    brought = [
        pltpu.make_async_copy(src, dst, in_s.at[at])
        for at, (src, dst) in enumerate(
            (
                (x_hbm, x_ref), (lw_hbm, lw_ref), (lg_hbm, lg_ref), (rw_hbm, rw_ref),
                (rg_hbm, rg_ref), (og_hbm, og_ref), (ow_hbm, ow_ref), (gain_hbm, gain_ref),
            )
        )
    ]
    for copy in brought:
        copy.start()

    barrier = pltpu.get_barrier_semaphore()
    for dp in range(n_p):
        for dq in range(n_q):
            if (dp, dq) != (0, 0):
                pl.semaphore_signal(
                    barrier, inc=1, device_id=(p ^ dp, q ^ dq), device_id_type=MESH
                )

    def pair_rows(k):
        return jnp.concatenate([x_ref[k], x_ref[k + rows]], axis=0)

    def factor(w_ref, g_ref, send):
        both = jnp.concatenate([w_ref[...].T, g_ref[...].T], axis=0)

        def step(k, _):
            pr = nt(both, pair_rows(k))
            turn[pl.ds(k, channels, stride=SUB), :] = pr[:channels] * jax.nn.sigmoid(pr[channels:])
            return 0

        lax.fori_loop(0, rows, step, 0, unroll=UF)

        def cast(e, _):
            at = pl.multiple_of(e * per * SUB, per * SUB)
            send[e] = turn[pl.ds(at, per * SUB), :].astype(BF16)
            return 0

        lax.fori_loop(0, n_p, cast, 0, unroll=2)

    def remote(src, dst, send_sem, recv_sem, to):
        return pltpu.make_async_remote_copy(
            src_ref=src, dst_ref=dst, send_sem=send_sem, recv_sem=recv_sem,
            device_id=to, device_id_type=MESH,
        )

    def arrived(ref, sem):
        remote(ref, ref, sem, sem, (p, q)).wait_recv()

    def left(ref, sem):
        remote(ref, ref, sem, sem, (p, q)).wait_send()

    def spread(kind, send, buf, order):
        def give(dp, lines, at):
            remote(
                send.at[p ^ dp, lines], buf.at[0, dp, lines],
                a_ss.at[kind], a_rs.at[kind, at], (p ^ dp, q),
            ).start()

        give(1, slice(None), n_c)
        for c in order:
            for dp in range(n_p - 1, 1, -1):
                give(dp, part[c], c)

    def own(buf, slot_from, slot_to, at, to, slots, lines=slice(None), sem=None):
        remote(
            buf.at[slot_from, slots, lines], buf.at[slot_to, slots, lines],
            f_ss.at[at], own_rs.at[at if sem is None else sem], to,
        ).start()

    def pass_on(buf, slot_from, slot_to, at, c, to):
        remote(
            buf.at[slot_from, away, part[c]], buf.at[slot_to, away, part[c]],
            f_ss.at[at], f_rs.at[at, c], to,
        ).start()

    def to_end(slot_from, slot_to, c):
        remote(
            lbuf.at[slot_from, :, part[c]], lbuf.at[slot_to, :, part[c]],
            e_ss, e_rs.at[slot_to, c], (p, end),
        ).start()

    for copy in brought:
        copy.wait()
    factor(lw_ref, lg_ref, lsend)
    pl.semaphore_wait(barrier, n_p * n_q - 1)
    spread(0, lsend, lbuf, range(n_c))
    lbuf[0, 0] = lsend[p]

    @pl.when(at_mid)
    def _():
        own(lbuf, 0, 2, 2, (p, far_mid), 0)

    @pl.when(jnp.logical_not(at_mid))
    def _():
        own(lbuf, 0, 1, 0, (p, mid), 0)

    factor(rw_ref, rg_ref, rsend)
    rbuf[0, 0] = rsend[p]
    spread(1, rsend, rbuf, (*range(n_h, n_c), *range(n_h)))

    def make_gate(k, _):
        gate[k] = jax.nn.sigmoid(
            jnp.dot(pair_rows(k), og_ref[...], preferred_element_type=F32)
        )
        return 0

    def gates():
        lax.fori_loop(0, rows, make_gate, 0, unroll=4)

    low = lax.broadcasted_iota(jnp.int32, (SUB, LANES), 1) < width

    def multiply(g, c, plane, sides):
        def products(d, _):
            at = pl.ds(pl.multiple_of(d * SUB, SUB), SUB)
            lines = lbuf[g, :, at, :].reshape(n_p * SUB, LANES)
            right = [rbuf[j, :, at, :].reshape(n_p * SUB, LANES) for j in range(sides)]
            sums = tn(lines, right[0] if sides == 1 else jnp.concatenate(right, axis=1))
            for j in range(sides):
                acc = sums[:, j * LANES : (j + 1) * LANES]
                for b in range(2):
                    top = b * 2 * SUB
                    a0, c0 = acc[top : top + SUB], acc[top + SUB : top + 2 * SUB]
                    b0 = acc[width + top : width + top + SUB]
                    d0 = acc[width + top + SUB : width + top + 2 * SUB]
                    tile = jnp.where(low, a0, d0) + pltpu.roll(
                        jnp.where(low, c0, b0), width, 1
                    )
                    osend[g, b, j, at, :] = (tile * count ** (-0.5)).astype(BF16)
            return 0

        first = sum(CHUNKS[:c])
        lax.fori_loop(first, first + CHUNKS[c], products, 0, unroll=CHUNKS[c])
        done = o_rs.at[0 if c < n_h else 1]
        for b in range(2):
            to_p = plane * 2 + b
            if sides == 2:
                remote(
                    osend.at[g, b, 1, part[c]], orecv.at[p, part[c]],
                    o_ss.at[1], done, (to_p, end),
                ).start()

            @pl.when(to_p != p)
            def _():
                remote(
                    osend.at[g, b, 0, part[c]], orecv.at[p, part[c]],
                    o_ss.at[0], done, (to_p, q),
                ).start()

            @pl.when(to_p == p)
            def _():
                orecv[p, part[c]] = osend[g, b, 0, part[c]]

    turn_of = p // 2

    def rotated(n, c, plane_of, sides):
        for t in range(n):
            g = lax.rem(turn_of + t, n)
            plane = plane_of[n - 1]
            for at in range(n - 1):
                plane = jnp.where(g == at, plane_of[at], plane)
            multiply(g, c, plane, sides)

    @pl.when(jnp.logical_not(at_mid))
    def _():
        def pass_left(c):
            arrived(lbuf.at[0, away, part[c]], a_rs.at[0, c])
            pass_on(lbuf, 0, 1, 0, c, (p, mid))

        def pass_right(c):
            arrived(rbuf.at[0, away, part[c]], a_rs.at[1, c])
            pass_on(rbuf, 0, 1, 1, c, (p, mid))

        arrived(lbuf.at[0, 1], a_rs.at[0, n_c])
        own(lbuf, 0, 1, 0, (p, mid), 1, sem=4)
        pass_left(0)
        arrived(rbuf.at[0, 1], a_rs.at[1, n_c])
        for c in range(1, n_h):
            pass_left(c)
        own(rbuf, 0, 1, 1, (p, mid), pair, moved)
        pass_left(n_h)
        for c in range(n_h, n_c):
            pass_right(c)
            if c + 1 < n_c:
                pass_left(c + 1)
        gates()
        for c in range(n_h):
            arrived(rbuf.at[0, away, part[c]], a_rs.at[1, c])
            arrived(lbuf.at[1, :, part[c]], e_rs.at[1, c])
            arrived(lbuf.at[2, :, part[c]], e_rs.at[2, c])
            rotated(3, c, (end, mid, far_mid), 1)
        for c in range(n_h):
            arrived(lbuf.at[3, :, part[c]], e_rs.at[3, c])
            multiply(3, c, far_end, 1)
        left(lbuf.at[0], f_ss.at[0])
        left(lbuf.at[0, :, moved], f_ss.at[1])

    @pl.when(at_mid)
    def _():
        def pass_near(c):
            arrived(lbuf.at[0, away, part[c]], a_rs.at[0, c])
            pass_on(lbuf, 0, 2, 2, c, (p, far_mid))
            if c < n_h:
                to_end(0, 1, c)

        def pass_far(c):
            arrived(lbuf.at[1, away, part[c]], f_rs.at[0, c])
            pass_on(lbuf, 1, 3, 3, c, (p, far_mid))

        def came(c):
            if c == 0:
                arrived(lbuf.at[2, 0], own_rs.at[2])
                arrived(lbuf.at[2, 1], own_rs.at[5])
            arrived(lbuf.at[2, away, part[c]], f_rs.at[2, c])
            if c < n_h:
                to_end(2, 2, c)

        def near(c):
            if c == n_h:
                arrived(rbuf.at[1, pair, moved], own_rs.at[1])
            arrived(rbuf.at[0, away, part[c]], a_rs.at[1, c])
            if c >= n_h:
                arrived(rbuf.at[1, away, part[c]], f_rs.at[1, c])
            rotated(3, c, planes[:3], 1 if c < n_h else 2)

        def mate():
            arrived(lbuf.at[0, 1], a_rs.at[0, n_c])
            own(lbuf, 0, 2, 2, (p, far_mid), 1, sem=5)

        def onward():
            arrived(lbuf.at[1, 0], own_rs.at[0])
            arrived(lbuf.at[1, 1], own_rs.at[4])
            own(lbuf, 1, 3, 3, (p, far_mid), pair)

        def came_far(c):
            if c == 0:
                arrived(lbuf.at[3, pair], own_rs.at[3])
            arrived(lbuf.at[3, away, part[c]], f_rs.at[3, c])
            if c < n_h:
                to_end(3, 3, c)

        def last(c):
            multiply(3, c, far_end, 1 if c < n_h else 2)

        first_right = next(step for step in ORDER if step[0] == "P")
        act = {"N": pass_near, "F": pass_far, "C": came, "P": near, "D": came_far, "Q": last}
        alone = {"M": mate, "O": onward, "g": gates}
        for step in ORDER:
            if step == first_right:
                arrived(rbuf.at[0, 1], a_rs.at[1, n_c])
            if step in alone:
                alone[step]()
            else:
                act[step[0]](int(step[1:]))
        left(lbuf.at[0], f_ss.at[2])
        left(lbuf.at[0], f_ss.at[3])
        left(lbuf.at[pl.ds(1, 3), :, home], e_ss)

    gain = jnp.broadcast_to(gain_ref[...], (channels, channels)).T
    left(lbuf.at[0, others], a_ss.at[0])
    left(lbuf.at[0, others], a_ss.at[1])

    arrived(orecv.at[others, home], o_rs.at[0])

    @pl.when(at_mid)
    def _():
        arrived(orecv.at[others, moved], o_rs.at[1])

    @pl.when(jnp.logical_not(at_mid))
    def _():
        arrived(orecv.at[:, moved], o_rs.at[1])

    def widen(e, _):
        at = pl.multiple_of(e * per * SUB, per * SUB)
        turn[pl.ds(at, per * SUB), :] = orecv[e].astype(F32)
        return 0

    lax.fori_loop(0, n_p, widen, 0, unroll=2)

    def finish(k, _):
        v = turn[pl.ds(k, channels, stride=SUB), :]
        v = v - jnp.mean(v, axis=0, keepdims=True)
        v = v * lax.rsqrt(jnp.mean(v * v, axis=0, keepdims=True) + 1e-05) * gain
        res = (tn(v.astype(BF16), ow_ref[...]) * gate[k]).astype(BF16)
        out_ref[k] = res[:width]
        out_ref[k + rows] = res[width:]
        return 0

    lax.fori_loop(0, rows, finish, 0, unroll=UE)

    left(orecv.at[others, home], o_ss.at[0])

    @pl.when(at_mid)
    def _():
        left(orecv.at[others, moved], o_ss.at[0])
        left(orecv.at[:, moved], o_ss.at[1])


def fused(n_p, n_q, pair_array, lw, rw, lg, rg, gain, ow, og):
    channels = lw.shape[1]
    slab = channels // n_p * SUB
    rows = pair_array.shape[0] // 2
    dma = pltpu.SemaphoreType.DMA
    return pl.pallas_call(
        functools.partial(kernel, n_p, n_q),
        out_shape=pltpu.VMEM(pair_array.shape, BF16),
        in_specs=[pl.BlockSpec(memory_space=pltpu.HBM)] * 8,
        out_specs=pl.BlockSpec(memory_space=pltpu.VMEM),
        scratch_shapes=[
            pltpu.VMEM(pair_array.shape, BF16),
            *[pltpu.VMEM(lw.shape, BF16)] * 4,
            pltpu.VMEM((1, channels), F32),
            pltpu.VMEM(ow.shape, BF16),
            pltpu.VMEM(og.shape, BF16),
            dma((8,)),
            pltpu.VMEM((channels * SUB, LANES), F32),
            pltpu.VMEM((n_p, slab, LANES), BF16),
            pltpu.VMEM((n_p, slab, LANES), BF16),
            pltpu.VMEM((4, n_p, slab, LANES), BF16),
            pltpu.VMEM((2, n_p, slab, LANES), BF16),
            pltpu.VMEM((4, 2, 2, slab, LANES), BF16),
            pltpu.VMEM((n_p, slab, LANES), BF16),
            pltpu.VMEM((rows, LANES, channels), F32),
            dma((2,)),
            dma((2, len(CHUNKS) + 1)),
            dma((4,)),
            dma((6,)),
            dma((4, len(CHUNKS))),
            dma(()),
            dma((4, len(HOME))),
            dma((2,)),
            dma((2,)),
        ],
        compiler_params=pltpu.CompilerParams(
            collective_id=0, has_side_effects=True, vmem_limit_bytes=33_554_432
        ),
    )(*(
        pltpu.with_memory_space_constraint(a, pltpu.HBM)
        for a in (pair_array, lw, rw, lg, rg, gain.reshape(1, channels), ow, og)
    ))


def solution(mesh):
    n_p, n_q = mesh.shape["pr"], mesh.shape["pc"]

    def on_device(pair_array, lw, *rest):
        first, second, wide = pair_array.shape
        fits = (
            n_q == 4
            and first == 2 * SUB
            and second == 2 * first
            and n_p == 2 * n_q
            and 2 * second == LANES
            and wide == LANES
            and lw.shape[1] == LANES
            and n_p * sum(CHUNKS) == LANES
        )
        if fits:
            return fused(n_p, n_q, pair_array, lw, *rest)
        return plain(pair_array, lw, *rest)

    return jax.shard_map(
        on_device,
        mesh=mesh,
        in_specs=(P("pr", "pc", None), P(), P(), P(), P(), P(), P(), P()),
        out_specs=P("pr", "pc", None),
        check_vma=False,
    )
```

time: 40.3 us -> 35.6 us (0.88); the launches traced: 40.1 us -> 34.9 us
  Pallas kernels: 39.3 us -> 34.1 us
    pallas_call x1, Pallas kernels: 39.3 us -> 34.1 us  [fused(): pl.pallas_call(functools.partial(kernel, n_p, n_q), out_shape=pltpu.VMEM(...]
where the time goes in v2:
time: 35.6 us; the launch traced here: 34.9 us
  Pallas kernels  34.1 us (96%)
  local copies, waits for them, and re-layouts  0.8 us (2%)
    pallas_call x1, Pallas kernels, fused(): pl.pallas_call(functools.partial(kernel, n_p, n_q), out_shape=pltpu.VMEM(...  34.1 us
    unnamed x1, local copies, waits for them, and re-layouts  0.8 us

profile of v2, /device:TPU:7, one launch (start us, length us, event | category | flops | bytes accessed | tf_op | source)
XLA Modules:
  0.0 34.9 jit_solution(7259029603980991322)
XLA Ops:
  0.0 34.1 %shard_map.82 = bf16[32,64,128]{2,1,0:T(8,128)(2,1)S(1)} custom-call(bf16[32,64,128]{2,1,0:T(8,128)(2,1)} %x_hbm.1, bf16[128,128]{1,0:T(8,128)(2,1)} %lw_hbm.1, bf16[128,128]{1,0:T(8,128)(2,1)} %rw_hbm.1, bf16[128,128]{1,0:T(8,128)(2,1)} %lg_hbm.1, bf16[128,128]{1,0:T(8,128)(2,1)} %rg_hbm.1, f32[1,128]{1,0:T(1,128)} %bitcast.1, bf16[128,128]{1,0:T(8,128)(2,1)} %ow_hbm.1, ...), custom_call_target="tpu_custom_call" | custom-call | tf_op jit(solution)/shard_map/pallas_call | solution.py:412
  34.1 0.8 %copy.10 = bf16[32,64,128]{2,1,0:T(8,128)(2,1)} copy(bf16[32,64,128]{2,1,0:T(8,128)(2,1)S(1)} %shard_map.82) | data formatting | bytes 1048576

commit v3 on v2

--- a/solution.py
+++ b/solution.py
@@ -76,7 +76,9 @@
 HOME = (3, 3)
 MOVED = (4, 4, 2)
 CHUNKS = HOME + MOVED
-ORDER = ('M', 'N0', 'N1', 'O', 'g', 'F0', 'N2', 'C0', 'F1', 'N3', 'C1', 'N4', 'F2', 'D0', 'P0', 'Q0', 'C2', 'P2', 'D1', 'P1', 'Q1', 'F3', 'C3', 'P3', 'F4', 'D2', 'Q2', 'C4', 'P4', 'D3', 'Q3', 'D4', 'Q4')
+ORDER = ('M', 'N0', 'N1', 'O', 'T0', 'T1', 'g', 'F0', 'N2', 'C0', 'F1', 'N3', 'C1', 'N4', 'F2', 'D0', 'P0', 'Q0', 'P2', 'C2', 'G2', 'D1', 'P1', 'Q1', 'F3', 'P3', 'C3', 'G3', 'F4', 'P4', 'D2', 'Q2', 'C4', 'G4', 'D3', 'Q3', 'D4', 'Q4')
+END_ORDER = ('L0', 'L1', 'B', 'L2', 'R2', 'L3', 'R3', 'L4', 'R4')
+WHOLE = tuple(c for c in range(len(CHUNKS)) if f"G{c}" not in ORDER)
 
 
 def kernel(
@@ -119,12 +121,17 @@
         copy.start()
 
     barrier = pltpu.get_barrier_semaphore()
-    for dp in range(n_p):
-        for dq in range(n_q):
-            if (dp, dq) != (0, 0):
-                pl.semaphore_signal(
-                    barrier, inc=1, device_id=(p ^ dp, q ^ dq), device_id_type=MESH
-                )
+    def greet(to):
+        pl.semaphore_signal(barrier, inc=1, device_id=to, device_id_type=MESH)
+
+    for dp in range(1, n_p):
+        greet((p ^ dp, q))
+
+    @pl.when(at_mid)
+    def _():
+        greet((p, far_mid))
+        greet((p, end))
+
 
     def pair_rows(k):
         return jnp.concatenate([x_ref[k], x_ref[k + rows]], axis=0)
@@ -191,7 +198,7 @@
     for copy in brought:
         copy.wait()
     factor(lw_ref, lg_ref, lsend)
-    pl.semaphore_wait(barrier, n_p * n_q - 1)
+    pl.semaphore_wait(barrier, n_p)
     spread(0, lsend, lbuf, range(n_c))
     lbuf[0, 0] = lsend[p]
 
@@ -281,16 +288,16 @@
 
         arrived(lbuf.at[0, 1], a_rs.at[0, n_c])
         own(lbuf, 0, 1, 0, (p, mid), 1, sem=4)
-        pass_left(0)
-        arrived(rbuf.at[0, 1], a_rs.at[1, n_c])
-        for c in range(1, n_h):
-            pass_left(c)
-        own(rbuf, 0, 1, 1, (p, mid), pair, moved)
-        pass_left(n_h)
-        for c in range(n_h, n_c):
-            pass_right(c)
-            if c + 1 < n_c:
-                pass_left(c + 1)
+
+        def right_pair():
+            arrived(rbuf.at[0, 1], a_rs.at[1, n_c])
+            own(rbuf, 0, 1, 1, (p, mid), pair, moved)
+
+        for step in END_ORDER:
+            if step == "B":
+                right_pair()
+            else:
+                {"L": pass_left, "R": pass_right}[step[0]](int(step[1:]))
         gates()
         for c in range(n_h):
             arrived(rbuf.at[0, away, part[c]], a_rs.at[1, c])
@@ -308,8 +315,6 @@
         def pass_near(c):
             arrived(lbuf.at[0, away, part[c]], a_rs.at[0, c])
             pass_on(lbuf, 0, 2, 2, c, (p, far_mid))
-            if c < n_h:
-                to_end(0, 1, c)
 
         def pass_far(c):
             arrived(lbuf.at[1, away, part[c]], f_rs.at[0, c])
@@ -329,7 +334,13 @@
             arrived(rbuf.at[0, away, part[c]], a_rs.at[1, c])
             if c >= n_h:
                 arrived(rbuf.at[1, away, part[c]], f_rs.at[1, c])
-            rotated(3, c, planes[:3], 1 if c < n_h else 2)
+            rotated(3 if c in WHOLE else 2, c, planes, 1 if c < n_h else 2)
+
+        def near_to_end(c):
+            to_end(0, 1, c)
+
+        def far_near(c):
+            multiply(2, c, far_mid, 1 if c < n_h else 2)
 
         def mate():
             arrived(lbuf.at[0, 1], a_rs.at[0, n_c])
@@ -351,7 +362,7 @@
             multiply(3, c, far_end, 1 if c < n_h else 2)
 
         first_right = next(step for step in ORDER if step[0] == "P")
-        act = {"N": pass_near, "F": pass_far, "C": came, "P": near, "D": came_far, "Q": last}
+        act = {"N": pass_near, "F": pass_far, "C": came, "P": near, "G": far_near, "T": near_to_end, "D": came_far, "Q": last}
         alone = {"M": mate, "O": onward, "g": gates}
         for step in ORDER:
             if step == first_right:

time: 35.6 us -> 34.3 us (0.963); the launches traced: 34.9 us -> 34.2 us
  Pallas kernels: 34.1 us -> 33.4 us
    pallas_call x1, Pallas kernels: 34.1 us -> 33.4 us  [fused(): pl.pallas_call(functools.partial(kernel, n_p, n_q), out_shape=pltpu.VMEM(...]
where the time goes in v3:
time: 34.3 us; the launch traced here: 34.2 us
  Pallas kernels  33.4 us (97%)
  local copies, waits for them, and re-layouts  0.8 us (2%)
    pallas_call x1, Pallas kernels, fused(): pl.pallas_call(functools.partial(kernel, n_p, n_q), out_shape=pltpu.VMEM(...  33.4 us
    unnamed x1, local copies, waits for them, and re-layouts  0.8 us

profile of v3, /device:TPU:7, one launch (start us, length us, event | category | flops | bytes accessed | tf_op | source)
XLA Modules:
  0.0 34.2 jit_solution(869267558556489667)
XLA Ops:
  0.0 33.4 %shard_map.82 = bf16[32,64,128]{2,1,0:T(8,128)(2,1)S(1)} custom-call(bf16[32,64,128]{2,1,0:T(8,128)(2,1)} %x_hbm.1, bf16[128,128]{1,0:T(8,128)(2,1)} %lw_hbm.1, bf16[128,128]{1,0:T(8,128)(2,1)} %rw_hbm.1, bf16[128,128]{1,0:T(8,128)(2,1)} %lg_hbm.1, bf16[128,128]{1,0:T(8,128)(2,1)} %rg_hbm.1, f32[1,128]{1,0:T(1,128)} %bitcast.1, bf16[128,128]{1,0:T(8,128)(2,1)} %ow_hbm.1, ...), custom_call_target="tpu_custom_call" | custom-call | tf_op jit(solution)/shard_map/pallas_call | solution.py:423
  33.4 0.8 %copy.10 = bf16[32,64,128]{2,1,0:T(8,128)(2,1)} copy(bf16[32,64,128]{2,1,0:T(8,128)(2,1)S(1)} %shard_map.82) | data formatting | bytes 1048576

commit v4 on v3

--- a/solution.py
+++ b/solution.py
@@ -12,6 +12,7 @@
 F32 = jnp.float32
 LANES = 128
 SUB = 16
+STEP = 17
 UF, UP, UE = 16, 8, 16
 
 
@@ -83,9 +84,9 @@
 
 def kernel(
     n_p, n_q, x_hbm, lw_hbm, rw_hbm, lg_hbm, rg_hbm, gain_hbm, ow_hbm, og_hbm, out_ref,
-    x_ref, lw_ref, rw_ref, lg_ref, rg_ref, gain_ref, ow_ref, og_ref, in_s,
+    x_ref, w_ref, gain_ref, x_s, w_s, gain_s,
     turn, lsend, rsend, lbuf, rbuf, osend, orecv, gate,
-    a_ss, a_rs, f_ss, own_rs, f_rs, e_ss, e_rs, o_ss, o_rs,
+    a_ss, a_rs, f_ss, own_rs, f_rs, e_ss, o_ss, o_rs,
 ):
     p = lax.axis_index("pr")
     q = lax.axis_index("pc")
@@ -108,17 +109,12 @@
     home = pl.ds(0, sum(HOME) * SUB)
     moved = pl.ds(sum(HOME) * SUB, sum(MOVED) * SUB)
 
-    brought = [
-        pltpu.make_async_copy(src, dst, in_s.at[at])
-        for at, (src, dst) in enumerate(
-            (
-                (x_hbm, x_ref), (lw_hbm, lw_ref), (lg_hbm, lg_ref), (rw_hbm, rw_ref),
-                (rg_hbm, rg_ref), (og_hbm, og_ref), (ow_hbm, ow_ref), (gain_hbm, gain_ref),
-            )
-        )
-    ]
-    for copy in brought:
-        copy.start()
+    bring_x = pltpu.make_async_copy(x_hbm, x_ref, x_s)
+    bring_gain = pltpu.make_async_copy(gain_hbm, gain_ref, gain_s)
+    bring_x.start()
+    for at, src in enumerate((lw_hbm, lg_hbm, rw_hbm, rg_hbm, og_hbm, ow_hbm)):
+        pltpu.make_async_copy(src, w_ref.at[at], w_s).start()
+    bring_gain.start()
 
     barrier = pltpu.get_barrier_semaphore()
     def greet(to):
@@ -136,19 +132,20 @@
     def pair_rows(k):
         return jnp.concatenate([x_ref[k], x_ref[k + rows]], axis=0)
 
-    def factor(w_ref, g_ref, send):
-        both = jnp.concatenate([w_ref[...].T, g_ref[...].T], axis=0)
+    def factor(first, send):
+        both = jnp.concatenate([w_ref[first].T, w_ref[first + 1].T], axis=0)
 
         def step(k, _):
             pr = nt(both, pair_rows(k))
-            turn[pl.ds(k, channels, stride=SUB), :] = pr[:channels] * jax.nn.sigmoid(pr[channels:])
+            turn[pl.ds(k, channels, stride=STEP), :] = pr[:channels] * jax.nn.sigmoid(pr[channels:])
             return 0
 
         lax.fori_loop(0, rows, step, 0, unroll=UF)
 
         def cast(e, _):
-            at = pl.multiple_of(e * per * SUB, per * SUB)
-            send[e] = turn[pl.ds(at, per * SUB), :].astype(BF16)
+            at = pl.multiple_of(e * per * STEP, per * STEP)
+            for d in range(per):
+                send[e, d * SUB : (d + 1) * SUB] = turn[pl.ds(at + d * STEP, SUB), :].astype(BF16)
             return 0
 
         lax.fori_loop(0, n_p, cast, 0, unroll=2)
@@ -169,7 +166,7 @@
         def give(dp, lines, at):
             remote(
                 send.at[p ^ dp, lines], buf.at[0, dp, lines],
-                a_ss.at[kind], a_rs.at[kind, at], (p ^ dp, q),
+                a_ss, a_rs.at[kind, at], (p ^ dp, q),
             ).start()
 
         give(1, slice(None), n_c)
@@ -177,27 +174,28 @@
             for dp in range(n_p - 1, 1, -1):
                 give(dp, part[c], c)
 
-    def own(buf, slot_from, slot_to, at, to, slots, lines=slice(None), sem=None):
+    def own(buf, slot_from, slot_to, at, to, slots, lines=slice(None)):
         remote(
             buf.at[slot_from, slots, lines], buf.at[slot_to, slots, lines],
-            f_ss.at[at], own_rs.at[at if sem is None else sem], to,
+            f_ss.at[at % 2], own_rs.at[at], to,
         ).start()
 
     def pass_on(buf, slot_from, slot_to, at, c, to):
         remote(
             buf.at[slot_from, away, part[c]], buf.at[slot_to, away, part[c]],
-            f_ss.at[at], f_rs.at[at, c], to,
+            f_ss.at[at % 2], f_rs.at[at, c], to,
         ).start()
 
     def to_end(slot_from, slot_to, c):
         remote(
             lbuf.at[slot_from, :, part[c]], lbuf.at[slot_to, :, part[c]],
-            e_ss, e_rs.at[slot_to, c], (p, end),
+            e_ss, f_rs.at[slot_to, c], (p, end),
         ).start()
 
-    for copy in brought:
-        copy.wait()
-    factor(lw_ref, lg_ref, lsend)
+    pltpu.make_async_copy(w_ref, w_ref, w_s).wait()
+    bring_gain.wait()
+    bring_x.wait()
+    factor(0, lsend)
     pl.semaphore_wait(barrier, n_p)
     spread(0, lsend, lbuf, range(n_c))
     lbuf[0, 0] = lsend[p]
@@ -210,13 +208,13 @@
     def _():
         own(lbuf, 0, 1, 0, (p, mid), 0)
 
-    factor(rw_ref, rg_ref, rsend)
+    factor(2, rsend)
     rbuf[0, 0] = rsend[p]
     spread(1, rsend, rbuf, (*range(n_h, n_c), *range(n_h)))
 
     def make_gate(k, _):
         gate[k] = jax.nn.sigmoid(
-            jnp.dot(pair_rows(k), og_ref[...], preferred_element_type=F32)
+            jnp.dot(pair_rows(k), w_ref[4], preferred_element_type=F32)
         )
         return 0
 
@@ -287,7 +285,7 @@
             pass_on(rbuf, 0, 1, 1, c, (p, mid))
 
         arrived(lbuf.at[0, 1], a_rs.at[0, n_c])
-        own(lbuf, 0, 1, 0, (p, mid), 1, sem=4)
+        own(lbuf, 0, 1, 0, (p, mid), 1)
 
         def right_pair():
             arrived(rbuf.at[0, 1], a_rs.at[1, n_c])
@@ -301,11 +299,11 @@
         gates()
         for c in range(n_h):
             arrived(rbuf.at[0, away, part[c]], a_rs.at[1, c])
-            arrived(lbuf.at[1, :, part[c]], e_rs.at[1, c])
-            arrived(lbuf.at[2, :, part[c]], e_rs.at[2, c])
+            arrived(lbuf.at[1, :, part[c]], f_rs.at[1, c])
+            arrived(lbuf.at[2, :, part[c]], f_rs.at[2, c])
             rotated(3, c, (end, mid, far_mid), 1)
         for c in range(n_h):
-            arrived(lbuf.at[3, :, part[c]], e_rs.at[3, c])
+            arrived(lbuf.at[3, :, part[c]], f_rs.at[3, c])
             multiply(3, c, far_end, 1)
         left(lbuf.at[0], f_ss.at[0])
         left(lbuf.at[0, :, moved], f_ss.at[1])
@@ -322,8 +320,7 @@
 
         def came(c):
             if c == 0:
-                arrived(lbuf.at[2, 0], own_rs.at[2])
-                arrived(lbuf.at[2, 1], own_rs.at[5])
+                arrived(lbuf.at[2, pair], own_rs.at[2])
             arrived(lbuf.at[2, away, part[c]], f_rs.at[2, c])
             if c < n_h:
                 to_end(2, 2, c)
@@ -344,11 +341,10 @@
 
         def mate():
             arrived(lbuf.at[0, 1], a_rs.at[0, n_c])
-            own(lbuf, 0, 2, 2, (p, far_mid), 1, sem=5)
+            own(lbuf, 0, 2, 2, (p, far_mid), 1)
 
         def onward():
-            arrived(lbuf.at[1, 0], own_rs.at[0])
-            arrived(lbuf.at[1, 1], own_rs.at[4])
+            arrived(lbuf.at[1, pair], own_rs.at[0])
             own(lbuf, 1, 3, 3, (p, far_mid), pair)
 
         def came_far(c):
@@ -371,13 +367,12 @@
                 alone[step]()
             else:
                 act[step[0]](int(step[1:]))
-        left(lbuf.at[0], f_ss.at[2])
-        left(lbuf.at[0], f_ss.at[3])
+        left(lbuf.at[0], f_ss.at[0])
+        left(lbuf.at[0], f_ss.at[1])
         left(lbuf.at[pl.ds(1, 3), :, home], e_ss)
 
     gain = jnp.broadcast_to(gain_ref[...], (channels, channels)).T
-    left(lbuf.at[0, others], a_ss.at[0])
-    left(lbuf.at[0, others], a_ss.at[1])
+    left(lbuf.at[pl.ds(0, 2), others], a_ss)
 
     arrived(orecv.at[others, home], o_rs.at[0])
 
@@ -390,17 +385,18 @@
         arrived(orecv.at[:, moved], o_rs.at[1])
 
     def widen(e, _):
-        at = pl.multiple_of(e * per * SUB, per * SUB)
-        turn[pl.ds(at, per * SUB), :] = orecv[e].astype(F32)
+        at = pl.multiple_of(e * per * STEP, per * STEP)
+        for d in range(per):
+            turn[pl.ds(at + d * STEP, SUB), :] = orecv[e, d * SUB : (d + 1) * SUB].astype(F32)
         return 0
 
     lax.fori_loop(0, n_p, widen, 0, unroll=2)
 
     def finish(k, _):
-        v = turn[pl.ds(k, channels, stride=SUB), :]
+        v = turn[pl.ds(k, channels, stride=STEP), :]
         v = v - jnp.mean(v, axis=0, keepdims=True)
         v = v * lax.rsqrt(jnp.mean(v * v, axis=0, keepdims=True) + 1e-05) * gain
-        res = (tn(v.astype(BF16), ow_ref[...]) * gate[k]).astype(BF16)
+        res = (tn(v.astype(BF16), w_ref[5]) * gate[k]).astype(BF16)
         out_ref[k] = res[:width]
         out_ref[k + rows] = res[width:]
         return 0
@@ -427,12 +423,12 @@
         out_specs=pl.BlockSpec(memory_space=pltpu.VMEM),
         scratch_shapes=[
             pltpu.VMEM(pair_array.shape, BF16),
-            *[pltpu.VMEM(lw.shape, BF16)] * 4,
+            pltpu.VMEM((6, *lw.shape), BF16),
             pltpu.VMEM((1, channels), F32),
-            pltpu.VMEM(ow.shape, BF16),
-            pltpu.VMEM(og.shape, BF16),
-            dma((8,)),
-            pltpu.VMEM((channels * SUB, LANES), F32),
+            dma(()),
+            dma(()),
+            dma(()),
+            pltpu.VMEM((channels * STEP, LANES), F32),
             pltpu.VMEM((n_p, slab, LANES), BF16),
             pltpu.VMEM((n_p, slab, LANES), BF16),
             pltpu.VMEM((4, n_p, slab, LANES), BF16),
@@ -440,13 +436,12 @@
             pltpu.VMEM((4, 2, 2, slab, LANES), BF16),
             pltpu.VMEM((n_p, slab, LANES), BF16),
             pltpu.VMEM((rows, LANES, channels), F32),
+            dma(()),
+            dma((2, len(CHUNKS) + 1)),
             dma((2,)),
-            dma((2, len(CHUNKS) + 1)),
             dma((4,)),
-            dma((6,)),
             dma((4, len(CHUNKS))),
             dma(()),
-            dma((4, len(HOME))),
             dma((2,)),
             dma((2,)),
         ],

time: 34.3 us -> 33.7 us (0.983)
  Pallas kernels: 33.4 us -> 32.8 us
    pallas_call x1, Pallas kernels: 33.4 us -> 32.8 us  [fused(): pl.pallas_call(functools.partial(kernel, n_p, n_q), out_shape=pltpu.VMEM(...]
where the time goes in v4:
time: 33.7 us; the launch traced here: 33.6 us
  Pallas kernels  32.8 us (97%)
  local copies, waits for them, and re-layouts  0.8 us (2%)
    pallas_call x1, Pallas kernels, fused(): pl.pallas_call(functools.partial(kernel, n_p, n_q), out_shape=pltpu.VMEM(...  32.8 us
    unnamed x1, local copies, waits for them, and re-layouts  0.8 us

profile of v4, /device:TPU:7, one launch (start us, length us, event | category | flops | bytes accessed | tf_op | source)
XLA Modules:
  0.0 33.6 jit_solution(14299942638945302990)
XLA Ops:
  0.0 32.8 %shard_map.82 = bf16[32,64,128]{2,1,0:T(8,128)(2,1)S(1)} custom-call(bf16[32,64,128]{2,1,0:T(8,128)(2,1)} %x_hbm.1, bf16[128,128]{1,0:T(8,128)(2,1)} %lw_hbm.1, bf16[128,128]{1,0:T(8,128)(2,1)} %rw_hbm.1, bf16[128,128]{1,0:T(8,128)(2,1)} %lg_hbm.1, bf16[128,128]{1,0:T(8,128)(2,1)} %rg_hbm.1, f32[1,128]{1,0:T(1,128)} %bitcast.1, bf16[128,128]{1,0:T(8,128)(2,1)} %ow_hbm.1, ...), custom_call_target="tpu_custom_call" | custom-call | tf_op jit(solution)/shard_map/pallas_call | solution.py:419
  32.8 0.8 %copy.10 = bf16[32,64,128]{2,1,0:T(8,128)(2,1)} copy(bf16[32,64,128]{2,1,0:T(8,128)(2,1)S(1)} %shard_map.82) | data formatting | bytes 1048576

commit v5 on v4

v5 whole, which is shorter than its diff:
```python
import functools

import jax
import jax.numpy as jnp
from jax import lax
from jax.experimental import pallas as pl
from jax.experimental.pallas import tpu as pltpu
from jax.sharding import PartitionSpec as P

MESH = pl.DeviceIdType.MESH
BF16 = jnp.bfloat16
F32 = jnp.float32
LANES = 128
SUB = 16
STEP = 17
UF, UP, UE = 16, 8, 16


def unit_channels(values, channel_gain):
    centred = values - jnp.mean(values, axis=-1, keepdims=True)
    return (
        centred
        * lax.rsqrt(jnp.mean(centred * centred, axis=-1, keepdims=True) + 1e-05)
        * channel_gain
    )


def make_factors(pair_in, left_weight, right_weight, left_gate, right_gate):
    left = jnp.einsum("ijc,cd->ijd", pair_in, left_weight, preferred_element_type=F32)
    left = left * jax.nn.sigmoid(
        jnp.einsum("ijc,cd->ijd", pair_in, left_gate, preferred_element_type=F32)
    )
    right = jnp.einsum("ijc,cd->ijd", pair_in, right_weight, preferred_element_type=F32)
    right = right * jax.nn.sigmoid(
        jnp.einsum("ijc,cd->ijd", pair_in, right_gate, preferred_element_type=F32)
    )
    return (pair_in, left.astype(BF16), right.astype(BF16))


def to_pair(mixed, ready, mid_gain, out_weight, out_gate):
    scaled = unit_channels(mixed.astype(F32), mid_gain).astype(BF16)
    scaled = lax.optimization_barrier(scaled)
    gate = jax.nn.sigmoid(jnp.einsum("ijc,cd->ijd", ready, out_gate, preferred_element_type=F32))
    return (
        jnp.einsum("ijd,dc->ijc", scaled, out_weight, preferred_element_type=F32) * gate
    ).astype(BF16)


def plain(
    pair_array, left_weight, right_weight, left_gate, right_gate, mid_gain, out_weight, out_gate
):
    ready, left, right = make_factors(pair_array, left_weight, right_weight, left_gate, right_gate)
    count = pair_array.shape[0] * lax.axis_size("pr")
    left_lines, right_lines = (
        lax.all_to_all(left, "pr", split_axis=2, concat_axis=0, tiled=True),
        lax.all_to_all(right, "pr", split_axis=2, concat_axis=0, tiled=True),
    )
    strip = jnp.einsum(
        "kid,kjd->ijd",
        lax.all_gather(left_lines, "pc", axis=1, tiled=True),
        right_lines,
        preferred_element_type=F32,
    )
    strip = (strip * count ** (-0.5)).astype(BF16)
    mixed = lax.all_to_all(strip, "pr", split_axis=0, concat_axis=2, tiled=True)
    return to_pair(mixed, ready, mid_gain, out_weight, out_gate)


def nt(a, b):
    return lax.dot_general(a, b, (((1,), (1,)), ((), ())), preferred_element_type=F32)


def tn(a, b):
    return lax.dot_general(a, b, (((0,), (0,)), ((), ())), preferred_element_type=F32)


HOME = (3, 3)
MOVED = (4, 3)
EDGE = (2, 4)
CHUNKS = tuple(HOME + MOVED + (edge,) for edge in EDGE)
COUNT = tuple(sum(sizes) for sizes in CHUNKS)
ORDER = ('M', 'N0', 'N1', 'O', 'T0', 'T1', 'g', 'F0', 'N2', 'C0', 'F1', 'N3', 'C1', 'N4', 'F2', 'D0', 'P0', 'Q0', 'P2', 'C2', 'G2', 'D1', 'P1', 'Q1', 'F3', 'P3', 'C3', 'G3', 'F4', 'P4', 'D2', 'Q2', 'C4', 'G4', 'D3', 'Q3', 'D4', 'Q4')
END_ORDER = ('L0', 'L1', 'B', 'L2', 'R2', 'L3', 'R3', 'L4', 'R4')
WHOLE = tuple(c for c in range(len(CHUNKS[0])) if f"G{c}" not in ORDER)


def kernel(
    n_p, n_q, x_hbm, lw_hbm, rw_hbm, lg_hbm, rg_hbm, gain_hbm, ow_hbm, og_hbm, out_ref,
    x_ref, w_ref, gain_ref, x_s, w_s, gain_s,
    turn, lsend, rsend, lbuf, rbuf, osend, orecv, gate,
    a_ss, a_rs, b_rs, f_ss, own_rs, f_rs, e_ss, o_ss, o_rs,
):
    p = lax.axis_index("pr")
    q = lax.axis_index("pc")
    half = q // 2
    mid, end = 1 + half, 3 * half
    far_mid, far_end = 2 - half, 3 - 3 * half
    at_mid = q == mid
    width = x_ref.shape[1]
    rows = x_ref.shape[0] // 2
    channels = w_ref.shape[2]
    count = n_p * x_ref.shape[0]
    planes = (mid, end, far_mid, far_end)
    n_c = len(CHUNKS[0])
    n_h = len(HOME)
    n_home = sum(HOME)
    parts = [
        [pl.ds(sum(sizes[:c]) * SUB, sizes[c] * SUB) for c in range(n_c)] for sizes in CHUNKS
    ]
    wholes = [pl.ds(0, n * SUB) for n in COUNT]
    moveds = [pl.ds(n_home * SUB, (n - n_home) * SUB) for n in COUNT]
    home = pl.ds(0, n_home * SUB)
    others = pl.ds(1, n_p - 1)
    pair = pl.ds(0, 2)
    away = pl.ds(2, n_p - 2)
    core = lax.rem(p, 2)

    def by_core(act):
        for k in range(2):

            @pl.when(core == k)
            def _():
                act(k)

    bring_x = pltpu.make_async_copy(x_hbm, x_ref, x_s)
    bring_gain = pltpu.make_async_copy(gain_hbm, gain_ref, gain_s)
    bring_x.start()
    for at, src in enumerate((lw_hbm, lg_hbm, rw_hbm, rg_hbm, og_hbm, ow_hbm)):
        pltpu.make_async_copy(src, w_ref.at[at], w_s).start()
    bring_gain.start()

    barrier = pltpu.get_barrier_semaphore()
    def greet(to):
        pl.semaphore_signal(barrier, inc=1, device_id=to, device_id_type=MESH)

    for dp in range(1, n_p):
        greet((p ^ dp, q))

    @pl.when(at_mid)
    def _():
        greet((p, far_mid))
        greet((p, end))


    def pair_rows(k):
        return jnp.concatenate([x_ref[k], x_ref[k + rows]], axis=0)

    def factor(first, send):
        both = jnp.concatenate([w_ref[first].T, w_ref[first + 1].T], axis=0)

        def step(k, _):
            pr = nt(both, pair_rows(k))
            turn[pl.ds(k, channels, stride=STEP), :] = pr[:channels] * jax.nn.sigmoid(pr[channels:])
            return 0

        lax.fori_loop(0, rows, step, 0, unroll=UF)

        def cast(e, _):
            for k in range(2):
                for d in range(COUNT[k]):
                    at = (e * sum(COUNT) + k * COUNT[0] + d) * STEP
                    send[e * 2 + k, d * SUB : (d + 1) * SUB] = turn[pl.ds(at, SUB), :].astype(BF16)
            return 0

        lax.fori_loop(0, n_p // 2, cast, 0)

    def remote(src, dst, send_sem, recv_sem, to):
        return pltpu.make_async_remote_copy(
            src_ref=src, dst_ref=dst, send_sem=send_sem, recv_sem=recv_sem,
            device_id=to, device_id_type=MESH,
        )

    def arrived(ref, sem):
        remote(ref, ref, sem, sem, (p, q)).wait_recv()

    def left(ref, sem):
        remote(ref, ref, sem, sem, (p, q)).wait_send()

    def spread(k, sems, send, buf, pieces):
        def give(dp, lines, sem):
            remote(
                send.at[p ^ dp, lines], buf.at[0, dp, lines],
                a_ss.at[dp & 1], sem, (p ^ dp, q),
            ).start()

        n = len(pieces[0])
        give(1, wholes[1 - k], sems.at[n])
        for at in range(n):
            for dp in range(n_p - 1, 1, -1):
                give(dp, pieces[k ^ (dp & 1)][at], sems.at[at])

    def own(buf, slot_from, slot_to, at, to, slots, lines):
        remote(
            buf.at[slot_from, slots, lines], buf.at[slot_to, slots, lines],
            f_ss.at[at % 2], own_rs.at[at], to,
        ).start()

    def to_end(slot_from, slot_to, c):
        remote(
            lbuf.at[slot_from, :, parts[0][c]], lbuf.at[slot_to, :, parts[0][c]],
            e_ss, f_rs.at[slot_to, c], (p, end),
        ).start()

    pltpu.make_async_copy(w_ref, w_ref, w_s).wait()
    bring_gain.wait()
    bring_x.wait()
    factor(0, lsend)
    pl.semaphore_wait(barrier, n_p)

    def send_left(k):
        lines = wholes[k]
        lbuf[0, 0, lines] = lsend[p, lines]

        @pl.when(at_mid)
        def _():
            own(lbuf, 0, 2, 2, (p, far_mid), 0, lines)

        @pl.when(jnp.logical_not(at_mid))
        def _():
            own(lbuf, 0, 1, 0, (p, mid), 0, lines)

        spread(k, a_rs, lsend, lbuf, parts)

    by_core(send_left)
    factor(2, rsend)

    def make_gate(k, _):
        gate[k] = jax.nn.sigmoid(
            jnp.dot(pair_rows(k), w_ref[4], preferred_element_type=F32)
        )
        return 0

    def gates():
        lax.fori_loop(0, rows, make_gate, 0, unroll=4)

    low = lax.broadcasted_iota(jnp.int32, (SUB, LANES), 1) < width

    def pass_on_core(k):
        sizes, part, whole, moved = CHUNKS[k], parts[k], wholes[k], moveds[k]

        rbuf[0, 0, whole] = rsend[p, whole]
        spread(k, b_rs, rsend, rbuf, [(*parts[n][n_h:], home) for n in range(2)])

        def pass_on(buf, slot_from, slot_to, at, c, to):
            remote(
                buf.at[slot_from, away, part[c]], buf.at[slot_to, away, part[c]],
                f_ss.at[at % 2], f_rs.at[at, c], to,
            ).start()

        def multiply(g, c, plane, sides):
            first = sum(sizes[:c])
            done = o_rs.at[0 if c < n_h else 1 + k]

            def some(these):
                def products(d, _):
                    at = pl.ds(pl.multiple_of(d * SUB, SUB), SUB)
                    lines = lbuf[g, :, at, :].reshape(n_p * SUB, LANES)
                    right = [rbuf[j, :, at, :].reshape(n_p * SUB, LANES) for j in these]
                    sums = tn(lines, right[0] if len(these) == 1 else jnp.concatenate(right, axis=1))
                    for n, j in enumerate(these):
                        acc = sums[:, n * LANES : (n + 1) * LANES]
                        for b in range(2):
                            top = b * 2 * SUB
                            a0, c0 = acc[top : top + SUB], acc[top + SUB : top + 2 * SUB]
                            b0 = acc[width + top : width + top + SUB]
                            d0 = acc[width + top + SUB : width + top + 2 * SUB]
                            tile = jnp.where(low, a0, d0) + pltpu.roll(
                                jnp.where(low, c0, b0), width, 1
                            )
                            osend[g, b, j, at, :] = (tile * count ** (-0.5)).astype(BF16)
                    return 0

                lax.fori_loop(first, first + sizes[c], products, 0, unroll=sizes[c])

            def give_end():
                for b in range(2):
                    remote(
                        osend.at[g, b, 1, part[c]], orecv.at[p, part[c]],
                        o_ss.at[1], done, (plane * 2 + b, end),
                    ).start()

            if sides == 2 and c == n_c - 1:
                some((1,))
                give_end()
                some((0,))
            else:
                some(tuple(range(sides)))
                if sides == 2:
                    give_end()
            for b in range(2):
                to_p = plane * 2 + b

                @pl.when(to_p != p)
                def _():
                    remote(
                        osend.at[g, b, 0, part[c]], orecv.at[p, part[c]],
                        o_ss.at[0], done, (to_p, q),
                    ).start()

                @pl.when(to_p == p)
                def _():
                    orecv[p, part[c]] = osend[g, b, 0, part[c]]

        turn_of = p // 2

        def rotated(n, c, plane_of, sides):
            for t in range(n):
                g = lax.rem(turn_of + t, n)
                plane = plane_of[n - 1]
                for at in range(n - 1):
                    plane = jnp.where(g == at, plane_of[at], plane)
                multiply(g, c, plane, sides)

        @pl.when(jnp.logical_not(at_mid))
        def _():
            def pass_left(c):
                arrived(lbuf.at[0, away, part[c]], a_rs.at[c])
                pass_on(lbuf, 0, 1, 0, c, (p, mid))

            def pass_right(c):
                arrived(rbuf.at[0, away, part[c]], b_rs.at[c - n_h])
                pass_on(rbuf, 0, 1, 1, c, (p, mid))

            arrived(lbuf.at[0, 1, whole], a_rs.at[n_c])
            own(lbuf, 0, 1, 0, (p, mid), 1, whole)

            def right_pair():
                arrived(rbuf.at[0, 1, whole], b_rs.at[n_c - n_h + 1])
                own(rbuf, 0, 1, 1, (p, mid), pair, moved)

            for step in END_ORDER:
                if step == "B":
                    right_pair()
                else:
                    {"L": pass_left, "R": pass_right}[step[0]](int(step[1:]))
            gates()
            for c in range(n_h):
                if c == 0:
                    arrived(rbuf.at[0, away, home], b_rs.at[n_c - n_h])
                arrived(lbuf.at[1, :, part[c]], f_rs.at[1, c])
                arrived(lbuf.at[2, :, part[c]], f_rs.at[2, c])
                rotated(3, c, (end, mid, far_mid), 1)
            for c in range(n_h):
                arrived(lbuf.at[3, :, part[c]], f_rs.at[3, c])
                multiply(3, c, far_end, 1)
            left(lbuf.at[0, :, whole], f_ss.at[0])
            left(lbuf.at[0, :, moved], f_ss.at[1])

        @pl.when(at_mid)
        def _():
            def pass_near(c):
                arrived(lbuf.at[0, away, part[c]], a_rs.at[c])
                pass_on(lbuf, 0, 2, 2, c, (p, far_mid))

            def pass_far(c):
                arrived(lbuf.at[1, away, part[c]], f_rs.at[0, c])
                pass_on(lbuf, 1, 3, 3, c, (p, far_mid))

            def came(c):
                if c == 0:
                    arrived(lbuf.at[2, pair, whole], own_rs.at[2])
                arrived(lbuf.at[2, away, part[c]], f_rs.at[2, c])
                if c < n_h:
                    to_end(2, 2, c)

            def near(c):
                if c == n_h:
                    arrived(rbuf.at[1, pair, moved], own_rs.at[1])
                if c == 0:
                    arrived(rbuf.at[0, away, home], b_rs.at[n_c - n_h])
                if c >= n_h:
                    arrived(rbuf.at[0, away, part[c]], b_rs.at[c - n_h])
                    arrived(rbuf.at[1, away, part[c]], f_rs.at[1, c])
                rotated(3 if c in WHOLE else 2, c, planes, 1 if c < n_h else 2)

            def near_to_end(c):
                to_end(0, 1, c)

            def far_near(c):
                multiply(2, c, far_mid, 1 if c < n_h else 2)

            def mate():
                arrived(lbuf.at[0, 1, whole], a_rs.at[n_c])
                own(lbuf, 0, 2, 2, (p, far_mid), 1, whole)

            def onward():
                arrived(lbuf.at[1, pair, whole], own_rs.at[0])
                own(lbuf, 1, 3, 3, (p, far_mid), pair, whole)

            def came_far(c):
                if c == 0:
                    arrived(lbuf.at[3, pair, whole], own_rs.at[3])
                arrived(lbuf.at[3, away, part[c]], f_rs.at[3, c])
                if c < n_h:
                    to_end(3, 3, c)

            def last(c):
                multiply(3, c, far_end, 1 if c < n_h else 2)

            first_right = next(step for step in ORDER if step[0] == "P")
            act = {"N": pass_near, "F": pass_far, "C": came, "P": near, "G": far_near, "T": near_to_end, "D": came_far, "Q": last}
            alone = {"M": mate, "O": onward, "g": gates}
            for step in ORDER:
                if step == first_right:
                    arrived(rbuf.at[0, 1, whole], b_rs.at[n_c - n_h + 1])
                if step in alone:
                    alone[step]()
                else:
                    act[step[0]](int(step[1:]))
            left(lbuf.at[0, :, whole], f_ss.at[0])
            left(lbuf.at[0, :, whole], f_ss.at[1])
            left(lbuf.at[pl.ds(1, 3), :, home], e_ss)

    by_core(pass_on_core)
    gain = jnp.broadcast_to(gain_ref[...], (channels, channels)).T

    def close(k):
        left(lbuf.at[pl.ds(0, 2), pl.ds(0, n_p // 2 - 1), wholes[k]], a_ss.at[0])
        left(lbuf.at[pl.ds(0, 2), pl.ds(0, n_p // 2), wholes[1 - k]], a_ss.at[1])
        arrived(orecv.at[others, home], o_rs.at[0])
        arrived(orecv.at[pl.ds(0, n_p // 2), moveds[1 - k]], o_rs.at[2 - k])

        @pl.when(at_mid)
        def _():
            arrived(orecv.at[pl.ds(0, n_p // 2 - 1), moveds[k]], o_rs.at[1 + k])

        @pl.when(jnp.logical_not(at_mid))
        def _():
            arrived(orecv.at[pl.ds(0, n_p // 2), moveds[k]], o_rs.at[1 + k])

    by_core(close)

    def widen(e, _):
        for k in range(2):
            for d in range(COUNT[k]):
                at = (e * sum(COUNT) + k * COUNT[0] + d) * STEP
                turn[pl.ds(at, SUB), :] = orecv[e * 2 + k, d * SUB : (d + 1) * SUB].astype(F32)
        return 0

    lax.fori_loop(0, n_p // 2, widen, 0)

    def finish(k, _):
        v = turn[pl.ds(k, channels, stride=STEP), :]
        v = v - jnp.mean(v, axis=0, keepdims=True)
        v = v * lax.rsqrt(jnp.mean(v * v, axis=0, keepdims=True) + 1e-05) * gain
        res = (tn(v.astype(BF16), w_ref[5]) * gate[k]).astype(BF16)
        out_ref[k] = res[:width]
        out_ref[k + rows] = res[width:]
        return 0

    lax.fori_loop(0, rows, finish, 0, unroll=UE)

    left(orecv.at[others, home], o_ss.at[0])

    def leave(k):
        left(orecv.at[others, moveds[k]], o_ss.at[0])
        left(orecv.at[:, moveds[k]], o_ss.at[1])

    @pl.when(at_mid)
    def _():
        by_core(leave)


def fused(n_p, n_q, pair_array, lw, rw, lg, rg, gain, ow, og):
    channels = lw.shape[1]
    slab = max(COUNT) * SUB
    rows = pair_array.shape[0] // 2
    dma = pltpu.SemaphoreType.DMA
    return pl.pallas_call(
        functools.partial(kernel, n_p, n_q),
        out_shape=pltpu.VMEM(pair_array.shape, BF16),
        in_specs=[pl.BlockSpec(memory_space=pltpu.HBM)] * 8,
        out_specs=pl.BlockSpec(memory_space=pltpu.VMEM),
        scratch_shapes=[
            pltpu.VMEM(pair_array.shape, BF16),
            pltpu.VMEM((6, *lw.shape), BF16),
            pltpu.VMEM((1, channels), F32),
            dma(()),
            dma(()),
            dma(()),
            pltpu.VMEM((channels * STEP, LANES), F32),
            pltpu.VMEM((n_p, slab, LANES), BF16),
            pltpu.VMEM((n_p, slab, LANES), BF16),
            pltpu.VMEM((4, n_p, slab, LANES), BF16),
            pltpu.VMEM((2, n_p, slab, LANES), BF16),
            pltpu.VMEM((4, 2, 2, slab, LANES), BF16),
            pltpu.VMEM((n_p, slab, LANES), BF16),
            pltpu.VMEM((rows, LANES, channels), F32),
            dma((2,)),
            dma((len(CHUNKS[0]) + 1,)),
            dma((len(MOVED) + 3,)),
            dma((2,)),
            dma((4,)),
            dma((4, len(CHUNKS[0]))),
            dma(()),
            dma((2,)),
            dma((3,)),
        ],
        compiler_params=pltpu.CompilerParams(
            collective_id=0, has_side_effects=True, vmem_limit_bytes=33_554_432
        ),
    )(*(
        pltpu.with_memory_space_constraint(a, pltpu.HBM)
        for a in (pair_array, lw, rw, lg, rg, gain.reshape(1, channels), ow, og)
    ))


def solution(mesh):
    n_p, n_q = mesh.shape["pr"], mesh.shape["pc"]

    def on_device(pair_array, lw, *rest):
        first, second, wide = pair_array.shape
        fits = (
            n_q == 4
            and first == 2 * SUB
            and second == 2 * first
            and n_p == 2 * n_q
            and 2 * second == LANES
            and wide == LANES
            and lw.shape[1] == LANES
            and n_p // 2 * sum(COUNT) == LANES
        )
        if fits:
            return fused(n_p, n_q, pair_array, lw, *rest)
        return plain(pair_array, lw, *rest)

    return jax.shard_map(
        on_device,
        mesh=mesh,
        in_specs=(P("pr", "pc", None), P(), P(), P(), P(), P(), P(), P()),
        out_specs=P("pr", "pc", None),
        check_vma=False,
    )
```

time: 33.7 us -> 33.4 us (level)
  Pallas kernels: 32.8 us -> 32.4 us
where the time goes in v5:
time: 33.4 us; the launch traced here: 33.3 us
  Pallas kernels  32.4 us (97%)
  local copies, waits for them, and re-layouts  0.8 us (2%)
    pallas_call x1, Pallas kernels, fused(): pl.pallas_call(functools.partial(kernel, n_p, n_q), out_shape=pltpu.VMEM(...  32.4 us
    unnamed x1, local copies, waits for them, and re-layouts  0.8 us

profile of v5, /device:TPU:7, one launch (start us, length us, event | category | flops | bytes accessed | tf_op | source)
XLA Modules:
  0.0 33.3 jit_solution(15863881816672608400)
XLA Ops:
  0.0 32.4 %shard_map.82 = bf16[32,64,128]{2,1,0:T(8,128)(2,1)S(1)} custom-call(bf16[32,64,128]{2,1,0:T(8,128)(2,1)} %x_hbm.1, bf16[128,128]{1,0:T(8,128)(2,1)} %lw_hbm.1, bf16[128,128]{1,0:T(8,128)(2,1)} %rw_hbm.1, bf16[128,128]{1,0:T(8,128)(2,1)} %lg_hbm.1, bf16[128,128]{1,0:T(8,128)(2,1)} %rg_hbm.1, f32[1,128]{1,0:T(1,128)} %bitcast.1, bf16[128,128]{1,0:T(8,128)(2,1)} %ow_hbm.1, ...), custom_call_target="tpu_custom_call" | custom-call | tf_op jit(solution)/shard_map/pallas_call | solution.py:469
  32.5 0.8 %copy.10 = bf16[32,64,128]{2,1,0:T(8,128)(2,1)} copy(bf16[32,64,128]{2,1,0:T(8,128)(2,1)S(1)} %shard_map.82) | data formatting | bytes 1048576

commit v6 on v5

--- a/solution.py
+++ b/solution.py
@@ -75,9 +75,8 @@
 
 
 HOME = (3, 3)
-MOVED = (4, 3)
-EDGE = (2, 4)
-CHUNKS = tuple(HOME + MOVED + (edge,) for edge in EDGE)
+MOVED = ((3, 3, 2), (4, 4, 4))
+CHUNKS = tuple(HOME + moved for moved in MOVED)
 COUNT = tuple(sum(sizes) for sizes in CHUNKS)
 ORDER = ('M', 'N0', 'N1', 'O', 'T0', 'T1', 'g', 'F0', 'N2', 'C0', 'F1', 'N3', 'C1', 'N4', 'F2', 'D0', 'P0', 'Q0', 'P2', 'C2', 'G2', 'D1', 'P1', 'Q1', 'F3', 'P3', 'C3', 'G3', 'F4', 'P4', 'D2', 'Q2', 'C4', 'G4', 'D3', 'Q3', 'D4', 'Q4')
 END_ORDER = ('L0', 'L1', 'B', 'L2', 'R2', 'L3', 'R3', 'L4', 'R4')
@@ -488,7 +487,7 @@
             pltpu.VMEM((rows, LANES, channels), F32),
             dma((2,)),
             dma((len(CHUNKS[0]) + 1,)),
-            dma((len(MOVED) + 3,)),
+            dma((len(MOVED[0]) + 2,)),
             dma((2,)),
             dma((4,)),
             dma((4, len(CHUNKS[0]))),

time: 33.4 us -> 33 us (0.988)
    pallas_call x1, Pallas kernels: 32.4 us -> 32.1 us  [fused(): pl.pallas_call(functools.partial(kernel, n_p, n_q), out_shape=pltpu.VMEM(...]
where the time goes in v6:
time: 33 us; the launch traced here: 32.9 us
  Pallas kernels  32.1 us (97%)
  local copies, waits for them, and re-layouts  0.8 us (2%)
    pallas_call x1, Pallas kernels, fused(): pl.pallas_call(functools.partial(kernel, n_p, n_q), out_shape=pltpu.VMEM(...  32.1 us
    unnamed x1, local copies, waits for them, and re-layouts  0.8 us

profile of v6, /device:TPU:7, one launch (start us, length us, event | category | flops | bytes accessed | tf_op | source)
XLA Modules:
  0.0 32.9 jit_solution(4097621001234669272)
XLA Ops:
  0.0 32.1 %shard_map.82 = bf16[32,64,128]{2,1,0:T(8,128)(2,1)S(1)} custom-call(bf16[32,64,128]{2,1,0:T(8,128)(2,1)} %x_hbm.1, bf16[128,128]{1,0:T(8,128)(2,1)} %lw_hbm.1, bf16[128,128]{1,0:T(8,128)(2,1)} %rw_hbm.1, bf16[128,128]{1,0:T(8,128)(2,1)} %lg_hbm.1, bf16[128,128]{1,0:T(8,128)(2,1)} %rg_hbm.1, f32[1,128]{1,0:T(1,128)} %bitcast.1, bf16[128,128]{1,0:T(8,128)(2,1)} %ow_hbm.1, ...), custom_call_target="tpu_custom_call" | custom-call | tf_op jit(solution)/shard_map/pallas_call | solution.py:468
  32.1 0.8 %copy.10 = bf16[32,64,128]{2,1,0:T(8,128)(2,1)} copy(bf16[32,64,128]{2,1,0:T(8,128)(2,1)S(1)} %shard_map.82) | data formatting | bytes 1048576

commit v7 on v5

--- a/solution.py
+++ b/solution.py
@@ -76,8 +76,7 @@
 
 HOME = (3, 3)
 MOVED = (4, 3)
-EDGE = (2, 4)
-CHUNKS = tuple(HOME + MOVED + (edge,) for edge in EDGE)
+CHUNKS = (HOME + (3, 3, 1), HOME + (5, 4, 4))
 COUNT = tuple(sum(sizes) for sizes in CHUNKS)
 ORDER = ('M', 'N0', 'N1', 'O', 'T0', 'T1', 'g', 'F0', 'N2', 'C0', 'F1', 'N3', 'C1', 'N4', 'F2', 'D0', 'P0', 'Q0', 'P2', 'C2', 'G2', 'D1', 'P1', 'Q1', 'F3', 'P3', 'C3', 'G3', 'F4', 'P4', 'D2', 'Q2', 'C4', 'G4', 'D3', 'Q3', 'D4', 'Q4')
 END_ORDER = ('L0', 'L1', 'B', 'L2', 'R2', 'L3', 'R3', 'L4', 'R4')

time: 33.4 us -> 33 us (0.988)
  Pallas kernels: 32.4 us -> 32 us
    pallas_call x1, Pallas kernels: 32.4 us -> 32 us  [fused(): pl.pallas_call(functools.partial(kernel, n_p, n_q), out_shape=pltpu.VMEM(...]
where the time goes in v7:
time: 33 us; the launch traced here: 32.8 us
  Pallas kernels  32 us (97%)
  local copies, waits for them, and re-layouts  0.8 us (2%)
    pallas_call x1, Pallas kernels, fused(): pl.pallas_call(functools.partial(kernel, n_p, n_q), out_shape=pltpu.VMEM(...  32 us
    unnamed x1, local copies, waits for them, and re-layouts  0.8 us

profile of v7, /device:TPU:7, one launch (start us, length us, event | category | flops | bytes accessed | tf_op | source)
XLA Modules:
  0.0 32.8 jit_solution(7155725803693545624)
XLA Ops:
  0.0 32.0 %shard_map.82 = bf16[32,64,128]{2,1,0:T(8,128)(2,1)S(1)} custom-call(bf16[32,64,128]{2,1,0:T(8,128)(2,1)} %x_hbm.1, bf16[128,128]{1,0:T(8,128)(2,1)} %lw_hbm.1, bf16[128,128]{1,0:T(8,128)(2,1)} %rw_hbm.1, bf16[128,128]{1,0:T(8,128)(2,1)} %lg_hbm.1, bf16[128,128]{1,0:T(8,128)(2,1)} %rg_hbm.1, f32[1,128]{1,0:T(1,128)} %bitcast.1, bf16[128,128]{1,0:T(8,128)(2,1)} %ow_hbm.1, ...), custom_call_target="tpu_custom_call" | custom-call | tf_op jit(solution)/shard_map/pallas_call | solution.py:468
  32.0 0.8 %copy.10 = bf16[32,64,128]{2,1,0:T(8,128)(2,1)} copy(bf16[32,64,128]{2,1,0:T(8,128)(2,1)S(1)} %shard_map.82) | data formatting | bytes 1048576
